TPU v7x, 32 devices: a whole 2x2x4 slice. The times are simulated.
32 devices in a mesh: grp: 2 (over x), scen: 16 (over z, y, core).
Axes of the slice: x: 2, y: 2, z: 4, core: 2. Of those that a mesh axis runs over, the one named last changes fastest.
Arguments:
- shocks: bfloat16 [32768, 2048], P(('grp', 'scen')), parts along dimension 0, may hold values from -8 to 8
- factor_sens: bfloat16 [2048, 1024], replicated, may hold values from -0.13258252 to 0.13258252
- notional: float32 [1024], replicated, may hold values from -0.25 to 0.25
- moneyness: float32 [1024], replicated, may hold values from -2 to 2
- desk_entity: int32 [64], replicated, may hold values from 0 to 7
- scenario_counts: int32 [32], P(('grp', 'scen')), parts along dimension 0, may hold values from 256 to 1024, as said below
- candidate_ids: int32 [2048], P('grp'), parts along dimension 0, may hold values from 0 to 16383, as said below
Outputs:
- tail_losses: float32 [512], P('grp'), parts along dimension 0
- cand_entity: float32 [2048, 8], P(('grp', 'scen')), parts along dimension 0
There are 2 independent parts, one for each index of `grp`. A program takes and returns all parts, laid end to end along the dimension named above; an argument that names none is the same for every part. Nothing has to cross between parts.
Inputs may be any that keep to these rules, and one draw needn't show every extreme that they name: `scenario_counts`: every block has at least 256 valid scenarios; some block in every draw is full. `candidate_ids`: each id b * 1024 + j names a valid scenario: j is below scenario_counts[b].
All inputs are finite; a program needn't handle non-finite values.
Results may differ from a plain program's by a relative error of at most 0.0003.
Values sent between devices are 32-bit elements; how exact they have to be, the bound alone decides.
A program may use at most 128 MiB of HBM per device.

v0:
```python
import jax
import jax.numpy as jnp
from jax import lax
from jax.sharding import PartitionSpec as P

K = 64
INSTR = 16
ENT = 8
TOPK = 256


def price(rows, factor_sens, notional, moneyness):
    value = jnp.dot(rows, factor_sens, preferred_element_type=jnp.float32)
    inst = notional * (jax.nn.softplus(value + moneyness) - jax.nn.softplus(moneyness))
    return jnp.sum(inst.reshape(rows.shape[0], K, INSTR), axis=2)


def body(shocks, factor_sens, notional, moneyness, desk_entity, scenario_counts, candidate_ids):
    slots = shocks.shape[0]
    count = scenario_counts[0]
    block_rows = min(256, slots)
    turns = slots // block_rows

    def one_block(step, desk_all):
        start = step * block_rows

        def active(unused):
            rows = lax.dynamic_slice_in_dim(shocks, start, block_rows, 0)
            return price(rows, factor_sens, notional, moneyness)

        def skipped(unused):
            return jnp.zeros((block_rows, K), jnp.float32)

        piece = lax.cond(start < count, active, skipped, 0)
        return lax.dynamic_update_slice_in_dim(desk_all, piece, start, 0)

    desk_pnl = lax.fori_loop(0, turns, one_block, jnp.zeros((slots, K), jnp.float32))
    loss = -jnp.sum(desk_pnl, axis=1)
    valid = jnp.arange(slots, dtype=jnp.int32) < count
    local_top = lax.top_k(jnp.where(valid, loss, jnp.float32(-1e30)), TOPK)[0]
    every_list = lax.all_gather(local_top, "scen", axis=0, tiled=True)
    tail_losses = lax.top_k(every_list, TOPK)[0]
    local_ids = candidate_ids - lax.axis_index("scen") * slots
    owned = (local_ids >= 0) & (local_ids < slots)
    clipped = jnp.clip(local_ids, 0, slots - 1)
    onehot = (desk_entity[:, None] == jnp.arange(ENT, dtype=jnp.int32)[None, :]).astype(jnp.float32)
    cand_pnl = lax.psum_scatter(
        jnp.where(owned[:, None], jnp.take(desk_pnl, clipped, axis=0), jnp.float32(0.0)),
        "scen",
        scatter_dimension=0,
        tiled=True,
    )
    cand_entity = -jnp.dot(cand_pnl, onehot, precision=lax.Precision.HIGHEST)
    return (tail_losses, cand_entity)


def solution(mesh):
    return jax.shard_map(
        body,
        mesh=mesh,
        in_specs=(P(("grp", "scen"), None), P(), P(), P(), P(), P(("grp", "scen")), P("grp")),
        out_specs=(P("grp"), P(("grp", "scen"), None)),
        check_vma=False,
    )
```

profile of v0, /device:TPU:0, one launch (start us, length us, event | category | flops | bytes accessed | tf_op | source)
XLA Modules:
  0.0 105.4 jit_solution(15786896003439924886)
XLA Ops:
  7.2 0.0 reduce-scatter.2.cloned.1.call-start
  7.2 0.7 fusion.5
  7.9 0.7 compare_and_fusion.1
  8.6 19.5 %while.13 = (s32[]{:T(128)}, f32[1024,64]{0,1:T(8,128)S(1)}, s32[]{:T(128)}, f32[1024]{0:T(1024)}, bf16[1024,2048]{1,0:T(8,128)(2,1)}, /*index=5*/bf16[2048,1024...) while((s32[]{:T(128)}, f32[1024,64]{0,1:T(8,128)S(1)}, ...), condition=%wide.region_4.5_spmd, body=%wide.region_0.4_spmd.sunk | while | flops 1076353024 | bytes 9654531 | solution.py:37
  9.3 5.6 %conditional.2 = (f32[256,64]{0,1:T(8,128)S(1)}) conditional(s32[]{:T(128)} %convert_element_type.9, () %tuple.42, (f32[1024]{0:T(1024)}, s32[]{:T(128)}, bf16[1024,2048]{1,0:T(8,128)(2,1)}, bf16[2048,1024]{1,0:T(8,128)(2,1)}, f32[1024]{0:T(1024)}) %tuple.43), branch_computations={%region_1.0_spmd, %region_2.3_spmd} | conditional | flops 1076353024 | bytes 9523246 | solution.py:34
  9.3 0.7 compare_select_fusion.1
  10.0 4.3 %fusion.1 = f32[256,1024]{1,0:T(8,128)S(1)} fusion(bf16[2048,1024]{1,0:T(8,128)(2,1)} %get-tuple-element.137, bf16[1024,2048]{1,0:T(8,128)(2,1)} %get-tuple-element.135, s32[]{:T(128)S(6)} %select_n.27, f32[1024]{0:T(1024)S(1)} %compare_select_fusion.1, f32[1024]{0:T(1024)} %get-tuple-element.138, f32[1024]{0:T(1024)} %get-tuple-element.134), kind=kOutput, calls=%fused_computation.4 | convolution fusion | flops 1076101120 | bytes 6303748 | tf_op jit(solution)/shard_map/while/body/eval_jaxpr/cond/branch_1_fun/dot_general | solution.py:13
  14.3 0.3 copy.10
  14.7 0.2 bitcast_reduce_fusion
  15.5 5.6 %conditional.2 = (f32[256,64]{0,1:T(8,128)S(1)}) conditional(s32[]{:T(128)} %convert_element_type.9, () %tuple.42, (f32[1024]{0:T(1024)}, s32[]{:T(128)}, bf16[1024,2048]{1,0:T(8,128)(2,1)}, bf16[2048,1024]{1,0:T(8,128)(2,1)}, f32[1024]{0:T(1024)}) %tuple.43), branch_computations={%region_1.0_spmd, %region_2.3_spmd} | conditional | flops 1076353024 | bytes 9523246 | solution.py:34
  15.6 0.7 compare_select_fusion.1
  16.3 4.3 %fusion.1 = f32[256,1024]{1,0:T(8,128)S(1)} fusion(bf16[2048,1024]{1,0:T(8,128)(2,1)} %get-tuple-element.137, bf16[1024,2048]{1,0:T(8,128)(2,1)} %get-tuple-element.135, s32[]{:T(128)S(6)} %select_n.27, f32[1024]{0:T(1024)S(1)} %compare_select_fusion.1, f32[1024]{0:T(1024)} %get-tuple-element.138, f32[1024]{0:T(1024)} %get-tuple-element.134), kind=kOutput, calls=%fused_computation.4 | convolution fusion | flops 1076101120 | bytes 6303748 | tf_op jit(solution)/shard_map/while/body/eval_jaxpr/cond/branch_1_fun/dot_general | solution.py:13
  20.6 0.3 copy.10
  20.9 0.2 bitcast_reduce_fusion
  21.8 5.6 %conditional.2 = (f32[256,64]{0,1:T(8,128)S(1)}) conditional(s32[]{:T(128)} %convert_element_type.9, () %tuple.42, (f32[1024]{0:T(1024)}, s32[]{:T(128)}, bf16[1024,2048]{1,0:T(8,128)(2,1)}, bf16[2048,1024]{1,0:T(8,128)(2,1)}, f32[1024]{0:T(1024)}) %tuple.43), branch_computations={%region_1.0_spmd, %region_2.3_spmd} | conditional | flops 1076353024 | bytes 9523246 | solution.py:34
  21.8 0.7 compare_select_fusion.1
  22.5 4.3 %fusion.1 = f32[256,1024]{1,0:T(8,128)S(1)} fusion(bf16[2048,1024]{1,0:T(8,128)(2,1)} %get-tuple-element.137, bf16[1024,2048]{1,0:T(8,128)(2,1)} %get-tuple-element.135, s32[]{:T(128)S(6)} %select_n.27, f32[1024]{0:T(1024)S(1)} %compare_select_fusion.1, f32[1024]{0:T(1024)} %get-tuple-element.138, f32[1024]{0:T(1024)} %get-tuple-element.134), kind=kOutput, calls=%fused_computation.4 | convolution fusion | flops 1076101120 | bytes 6303748 | tf_op jit(solution)/shard_map/while/body/eval_jaxpr/cond/branch_1_fun/dot_general | solution.py:13
  26.8 0.3 copy.10
  27.2 0.2 bitcast_reduce_fusion
  28.1 0.0 copy-start
  28.1 0.2 copy.12
  28.3 2.8 %gather_fusion = f32[1024,64]{1,0:T(8,128)S(1)} fusion(f32[1024,64]{1,0:T(8,128)S(1)} %copy.12, s32[1024]{0:T(1024)S(1)} %fusion.5), kind=kCustom, calls=%fused_computation | custom fusion | bytes 528384 | tf_op jit(solution)/shard_map/jit(_take)/gather | solution.py:48
  31.2 1.1 %select_select_fusion = f32[1024,64]{1,0:T(8,128)} fusion(f32[1024,64]{1,0:T(8,128)S(1)} %gather_fusion, pred[1024]{0:T(1024)(128)(4,1)S(1)} %get-tuple-element.177, pred[1024]{0:T(1024)(128)(4,1)S(1)} %get-tuple-element.176), kind=kLoop, calls=%fused_computation.11 | loop fusion | flops 131072 | bytes 526336 | tf_op jit(solution)/shard_map/jit(_where)/select_n | solution.py:48
  32.3 0.0 reduce-scatter.2.cloned.1.call-update
  33.0 4.4 %top_k.14 = (f32[1024]{0:T(1024)S(1)}, s32[1024]{0:T(1024)}) sort(f32[1024]{0:T(1024)S(1)} %negate_select_fusion, s32[1024]{0:T(1024)S(1)} %iota.14), dimensions={0}, to_apply=%region_6.7 | sort | flops 10240 | bytes 16384 | tf_op jit(solution)/shard_map/top_k | solution.py:40
  37.4 25.6 %all-gather = f32[16,1,256]{2,1,0:T(1,128)S(1)} all-gather(f32[1,1,256]{2,1,0:T(1,128)S(1)} %bitcast.9), channel_id=1, replica_groups=mesh['grp'=2,'scen'=16] {'scen'}, dimensions={0}, use_global_device_ids=true | all-gather | bytes 17408 | tf_op jit(solution)/shard_map/all_gather | solution.py:41
  63.1 5.9 %top_k.20 = (f32[4096]{0:T(1024)S(1)}, s32[4096]{0:T(1024)}) sort(f32[4096]{0:T(1024)S(1)} %bitcast.8, s32[4096]{0:T(1024)S(1)} %iota.15), dimensions={0}, to_apply=%region_7.8 | sort | flops 49152 | bytes 65536 | tf_op jit(solution)/shard_map/top_k | solution.py:42
  69.0 0.6 top_k.21
  69.5 27.4 %reduce-scatter.2.cloned.1.call-done = f32[64,64]{1,0:T(8,128)} async-done(((f32[1024,64]{1,0:T(8,128)}), f32[64,64]{1,0:T(8,128)}) %reduce-scatter.2.cloned.1.call-update) | async-done | bytes 16400 | tf_op jit(solution)/shard_map/reduce_scatter | solution.py:47
  96.9 0.0 copy-done
  96.9 1.6 %convolution_negate_fusion = f32[64,8]{0,1:T(8,128)} fusion(f32[64,64]{1,0:T(8,128)} %reduce-scatter.2.cloned.1.call-done, s32[64]{0:T(128)S(1)} %copy-done), kind=kOutput, calls=%fused_computation.10 | convolution fusion | flops 394240 | bytes 18688 | tf_op jit(solution)/shard_map/dot_general | solution.py:53
  (12 shorter events, 0.1 us)
Async XLA Ops:
  7.2 89.8 %reduce-scatter.2.cloned.1.call-start = ((), (), s32[]{:S(2)}) async-start(), calls=%async_computation.1 | async-start | bytes 557056 | tf_op jit(solution)/shard_map/reduce_scatter | solution.py:47
  28.1 68.8 %copy-start = (s32[64]{0:T(128)S(1)}, s32[64]{0:T(128)}, u32[]{:S(2)}) copy-start(s32[64]{0:T(128)} %param.15) | copy-start | bytes 772
Sparse Core Ops, SparseCore 0:
  32.4 64.4 reduce-scatter.1
where the time goes:
time: 106 us; the launch traced here: 105 us
  waiting for transfers between devices  27.4 us (26%)
  blocking collectives  25.6 us (24%)
  other arithmetic  15.5 us (15%)
  between operations  14.7 us (14%)
  matrix products  14.5 us (14%)
  local copies, waits for them, and re-layouts  4.64 us (4%)
  loops' own time  2.88 us (3%)
    reduce_scatter x1, waiting for transfers between devices, body(): lax.psum_scatter(jnp.where(owned[:, None], jnp.take(desk_pnl, clipped, ax...  27.4 us
    all_gather x1, blocking collectives, body(): every_list = lax.all_gather(local_top, 'scen', axis=0, tiled=True)  25.6 us
    dot_general x3, matrix products, price(): value = jnp.dot(rows, factor_sens, preferred_element_type=jnp.float32)  12.9 us
    top_k x1, other arithmetic, body(): tail_losses = lax.top_k(every_list, TOPK)[0]  5.87 us
    top_k x1, other arithmetic, body(): local_top = lax.top_k(jnp.where(valid, loss, jnp.float32(-1e+30)), TOPK)[0]  4.43 us
    gather x1, local copies, waits for them, and re-layouts, body(): jnp.take(desk_pnl, clipped, axis=0)  2.81 us
    another operation x1, loops' own time, body(): lax.fori_loop(0, turns, one_block, jnp.zeros((slots, K), jnp.float32))  2.74 us
  transfers between devices with their start and end apart: 1, of which 1 were waited for; matrix products, arithmetic and copies ran while one was open for 10% of the time, Pallas kernels for 0%

commit v1 on v0

v1 whole, which is shorter than its diff:
```python
import functools

import jax
import jax.numpy as jnp
from jax import lax
from jax.experimental import pallas as pl
from jax.experimental.pallas import tpu as pltpu
from jax.sharding import PartitionSpec as P

INSTR = 16
ENT = 8
TOPK = 256
LANES = 128
BLOCK = 128
LOW = -1e30


def bitonic_sort(x, ascending):
    lane = lax.broadcasted_iota(jnp.int32, (x.shape[0], LANES), 1)
    parts = [x[:, p * LANES : (p + 1) * LANES] for p in range(TOPK // LANES)]
    a, b = parts
    big, small = jnp.maximum(a, b), jnp.minimum(a, b)
    parts = [jnp.where(ascending, small, big), jnp.where(ascending, big, small)]
    step = LANES // 2
    while step:
        first = (lane & step) == 0
        keep_big = first != ascending
        out = []
        for p in parts:
            other = jnp.where(first, pltpu.roll(p, LANES - step, 1), pltpu.roll(p, step, 1))
            out.append(jnp.where(keep_big, jnp.maximum(p, other), jnp.minimum(p, other)))
        parts = out
        step //= 2
    return jnp.concatenate(parts, axis=1)


def kernel(
    n,
    chunk,
    ent_ref,
    count_ref,
    shocks_hbm,
    sens_hbm,
    notional_ref,
    money_ref,
    ids_ref,
    tail_ref,
    cand_ref,
    shocks,
    sens,
    value,
    weight,
    sums,
    row_loss,
    col_loss,
    tail_send,
    tail_recv,
    cand_send,
    cand_recv,
    merged,
    flipped,
    x_sem,
    w_sem,
    tail_ssem,
    tail_rsem,
    cand_ssem,
    cand_rsem,
):
    slots, factors = shocks.shape
    cols = sens.shape[1]
    turns = slots // BLOCK
    me = lax.axis_index("scen")

    wcopies = []
    for q in range(4):
        width = cols // 4
        c = pltpu.make_async_copy(
            sens_hbm.at[:, pl.ds(q * width, width)], sens.at[:, pl.ds(q * width, width)], w_sem.at[q]
        )
        c.start()
        wcopies.append(c)

    def rows_copy(i):
        return pltpu.make_async_copy(
            shocks_hbm.at[pl.ds(i * BLOCK, BLOCK), :], shocks.at[pl.ds(i * BLOCK, BLOCK), :], x_sem.at[i]
        )

    for i in range(turns):
        rows_copy(i).start()

    barrier = pltpu.get_barrier_semaphore()
    for k in range(1, n):
        pl.semaphore_signal(barrier, inc=1, device_id={"scen": lax.rem(me + k, n)}, device_id_type=pl.DeviceIdType.MESH)

    wlane = lax.broadcasted_iota(jnp.int32, (INSTR, 2 * LANES), 1)
    for k in range(cols // INSTR):
        hit = (wlane == ent_ref[k]) | (wlane >= LANES)
        weight[k * INSTR : (k + 1) * INSTR, :] = jnp.where(hit, -1.0, 0.0).astype(jnp.bfloat16)

    money = money_ref[...]
    notional = notional_ref[...]
    base = jnp.maximum(money, 0.0) + jnp.log(1.0 + jnp.exp(-jnp.abs(money)))

    def matmul(i, slot):
        x = shocks[pl.ds(pl.multiple_of(i * BLOCK, BLOCK), BLOCK), :]
        value[slot] = jnp.dot(x, sens[...], preferred_element_type=jnp.float32)

    def finish(i, slot):
        z = value[slot] + money
        inst = notional * (jnp.maximum(z, 0.0) + jnp.log(1.0 + jnp.exp(-jnp.abs(z))) - base)
        hi = inst.astype(jnp.bfloat16)
        lo = (inst - hi.astype(jnp.float32)).astype(jnp.bfloat16)
        w = weight[...]
        total = jnp.dot(hi, w, preferred_element_type=jnp.float32) + jnp.dot(lo, w, preferred_element_type=jnp.float32)
        sums[pl.ds(pl.multiple_of(i * BLOCK, BLOCK), BLOCK), :] = total

    for c in wcopies:
        c.wait()
    rows_copy(0).wait()
    matmul(0, 0)

    def step(i, unused):
        rows_copy(i).wait()
        matmul(i, lax.rem(i, 2))
        finish(i - 1, lax.rem(i - 1, 2))
        return unused

    lax.fori_loop(1, turns, step, 0)
    finish(turns - 1, (turns - 1) % 2)

    count = count_ref[0]
    sub = lax.broadcasted_iota(jnp.int32, (LANES, LANES), 0)
    for t in range(slots // LANES):
        loss = sums[t * LANES : (t + 1) * LANES, LANES:]
        loss = jnp.where(sub + t * LANES < count, loss, LOW)
        col_loss[t * LANES : (t + 1) * LANES, :] = loss
        row_loss[:, t * LANES : (t + 1) * LANES] = loss.T[:8, :]
    rank = lax.broadcasted_iota(jnp.int32, (LANES, LANES), 1)
    order = lax.select(me >= n // 2, 1, 0)
    rank_lo = (rank + order * (TOPK - 1 - 2 * rank)).astype(jnp.float32)
    rank_hi = (rank + LANES + order * (TOPK - 1 - 2 * (rank + LANES))).astype(jnp.float32)
    ones = jnp.ones((LANES, LANES), jnp.bfloat16)

    def ranked(t, best):
        mine = col_loss[pl.ds(pl.multiple_of(t * LANES, LANES), LANES), :]
        larger = jnp.zeros((LANES, LANES), jnp.float32)
        for s in range(slots // LANES):
            theirs = row_loss[0:1, s * LANES : (s + 1) * LANES]
            larger = larger + jnp.where(theirs > mine, 1.0, 0.0)
        place = jnp.dot(larger.astype(jnp.bfloat16), ones, preferred_element_type=jnp.float32)
        b_lo, b_hi = best
        b_lo = jnp.minimum(b_lo, jnp.min(jnp.where(place <= rank_lo, mine, jnp.inf), axis=0, keepdims=True))
        b_hi = jnp.minimum(b_hi, jnp.min(jnp.where(place <= rank_hi, mine, jnp.inf), axis=0, keepdims=True))
        return b_lo, b_hi

    empty = jnp.full((1, LANES), jnp.inf, jnp.float32)
    b_lo, b_hi = lax.fori_loop(0, slots // LANES, ranked, (empty, empty))
    top = jnp.concatenate([b_lo, b_hi], axis=1)
    tail_send[...] = top
    tail_recv[me] = top

    pl.semaphore_wait(barrier, n - 1)

    def tail_copy(k):
        return pltpu.make_async_remote_copy(
            src_ref=tail_send,
            dst_ref=tail_recv.at[me],
            send_sem=tail_ssem.at[k],
            recv_sem=tail_rsem.at[k],
            device_id={"scen": lax.rem(me + k, n)},
            device_id_type=pl.DeviceIdType.MESH,
        )

    def cand_copy(k):
        peer = lax.rem(me + k, n)
        return pltpu.make_async_remote_copy(
            src_ref=cand_send.at[lax.div(peer * chunk, LANES)],
            dst_ref=cand_recv.at[me],
            send_sem=cand_ssem.at[k],
            recv_sem=cand_rsem.at[k],
            device_id={"scen": peer},
            device_id_type=pl.DeviceIdType.MESH,
        )

    for k in range(1, n):
        tail_copy(k).start()

    entity = jnp.concatenate(
        [sums[t * LANES : (t + 1) * LANES, :LANES].T[:ENT, :] for t in range(slots // LANES)], axis=1
    )
    hi = entity.astype(jnp.bfloat16)
    rest = entity - hi.astype(jnp.float32)
    mid = rest.astype(jnp.bfloat16)
    lo = (rest - mid.astype(jnp.float32)).astype(jnp.bfloat16)
    split = jnp.concatenate([hi.astype(jnp.float32), mid.astype(jnp.float32), lo.astype(jnp.float32)], axis=0)
    split = split.astype(jnp.bfloat16)
    width = 2 * LANES
    for q in range(ids_ref.shape[1] // width):
        local = ids_ref[:, q * width : (q + 1) * width] - me * slots
        hot = lax.broadcasted_iota(jnp.int32, (slots, width), 0) == local
        hot = jnp.where(hot, 1.0, 0.0).astype(jnp.bfloat16)
        got = jnp.dot(split, hot, preferred_element_type=jnp.float32)
        got = got[:ENT] + got[ENT : 2 * ENT] + got[2 * ENT :]
        for h in range(width // LANES):
            cand_send[q * (width // LANES) + h] = got[:, h * LANES : (h + 1) * LANES]
    mine_block = lax.div(me * chunk, LANES)
    cand_recv[me] = cand_send[mine_block]
    for k in range(1, n):
        cand_copy(k).start()

    for k in range(1, n):
        tail_copy(k).wait_recv()
    for b in range(n):
        merged[b : b + 1, :] = tail_recv[b]
    lists = n
    while lists > 1:
        half = lists // 2
        if lists == n:
            x = merged[...]
        x = jnp.maximum(x[:half], x[half : 2 * half])
        pad = max(half, 8)
        if half < 8:
            x = jnp.concatenate([x] * (pad // half), axis=0)
        row = lax.broadcasted_iota(jnp.int32, (pad, LANES), 0)
        ascending = row >= (half // 2 if half > 1 else pad)
        x = bitonic_sort(x, ascending)
        lists = half
    tail_ref[...] = x[:1, :]

    for k in range(1, n):
        cand_copy(k).wait_recv()
    total = cand_recv[0]
    for b in range(1, n):
        total = total + cand_recv[b]
    square = jnp.concatenate([total, jnp.zeros((LANES - ENT, LANES), jnp.float32)], axis=0)
    flipped[...] = square.T
    offset = lax.rem(me * chunk, LANES)
    cand_ref[...] = flipped[pl.ds(pl.multiple_of(offset, 8), chunk), :ENT]
    for k in range(1, n):
        tail_copy(k).wait_send()
        cand_copy(k).wait_send()


def body(n, shocks, factor_sens, notional, moneyness, desk_entity, scenario_counts, candidate_ids):
    slots, factors = shocks.shape
    cols = factor_sens.shape[1]
    cands = candidate_ids.shape[0]
    chunk = cands // n
    vmem = pl.BlockSpec(memory_space=pltpu.VMEM)
    smem = pl.BlockSpec(memory_space=pltpu.SMEM)
    hbm = pl.BlockSpec(memory_space=pl.ANY)
    tail, cand = pl.pallas_call(
        functools.partial(kernel, n, chunk),
        out_shape=(
            jax.ShapeDtypeStruct((1, TOPK), jnp.float32),
            jax.ShapeDtypeStruct((chunk, ENT), jnp.float32),
        ),
        in_specs=[smem, smem, hbm, hbm, vmem, vmem, vmem],
        out_specs=(vmem, vmem),
        scratch_shapes=[
            pltpu.VMEM((slots, factors), jnp.bfloat16),
            pltpu.VMEM((factors, cols), jnp.bfloat16),
            pltpu.VMEM((2, BLOCK, cols), jnp.float32),
            pltpu.VMEM((cols, 2 * LANES), jnp.bfloat16),
            pltpu.VMEM((slots, 2 * LANES), jnp.float32),
            pltpu.VMEM((8, slots), jnp.float32),
            pltpu.VMEM((slots, LANES), jnp.float32),
            pltpu.VMEM((1, TOPK), jnp.float32),
            pltpu.VMEM((n, 1, TOPK), jnp.float32),
            pltpu.VMEM((cands // LANES, ENT, LANES), jnp.float32),
            pltpu.VMEM((n, ENT, LANES), jnp.float32),
            pltpu.VMEM((n, TOPK), jnp.float32),
            pltpu.VMEM((LANES, LANES), jnp.float32),
            pltpu.SemaphoreType.DMA((slots // BLOCK,)),
            pltpu.SemaphoreType.DMA((4,)),
            pltpu.SemaphoreType.DMA((n,)),
            pltpu.SemaphoreType.DMA((n,)),
            pltpu.SemaphoreType.DMA((n,)),
            pltpu.SemaphoreType.DMA((n,)),
        ],
        compiler_params=pltpu.CompilerParams(
            collective_id=0, has_side_effects=True, vmem_limit_bytes=48 * 1024 * 1024
        ),
    )(
        desk_entity,
        scenario_counts,
        shocks,
        factor_sens,
        notional.reshape(1, cols),
        moneyness.reshape(1, cols),
        candidate_ids.reshape(1, cands),
    )
    return tail.reshape(TOPK), cand


def solution(mesh):
    return jax.shard_map(
        functools.partial(body, mesh.shape["scen"]),
        mesh=mesh,
        in_specs=(P(("grp", "scen"), None), P(), P(), P(), P(), P(("grp", "scen")), P("grp")),
        out_specs=(P("grp"), P(("grp", "scen"), None)),
        check_vma=False,
    )
```

time: 106 us -> 32.9 us (0.31)
  waiting for transfers between devices: 27.4 us -> 0 us
  blocking collectives: 25.6 us -> 0 us
  Pallas kernels: 0 us -> 25.2 us
  other arithmetic: 15.5 us -> 0 us
  matrix products: 14.5 us -> 0 us
  between operations: 14.7 us -> 1.3 us
  loops' own time: 2.88 us -> 0 us
  local copies, waits for them, and re-layouts: 4.64 us -> 6.12 us
    reduce_scatter x1 -> x0, waiting for transfers between devices: 27.4 us -> none  [body(): lax.psum_scatter(jnp.where(owned[:, None], jnp.take(desk_pnl, clipped, ax...]
    all_gather x1 -> x0, blocking collectives: 25.6 us -> none  [body(): every_list = lax.all_gather(local_top, 'scen', axis=0, tiled=True)]
    pallas_call x0 -> x1, Pallas kernels: none -> 25.2 us  [body(): pl.pallas_call(functools.partial(kernel, n, chunk), out_shape=(jax.ShapeD...]
    dot_general x4 -> x0, matrix products: 14.5 us -> none  [the longest x3 12.9 us: price(): value = jnp.dot(rows, factor_sens, preferred_element_type=jnp.float32)]
    top_k x2 -> x0, other arithmetic: 10.3 us -> none  [the longest x1 5.87 us: body(): tail_losses = lax.top_k(every_list, TOPK)[0]]
    unnamed x2 -> x12, local copies, waits for them, and re-layouts: 0.01 us -> 6.12 us
    select_n x5 -> x0, other arithmetic: 3.23 us -> none  [the longest x3 2.1 us: price(): jax.nn.softplus(moneyness)]
    another operation x5 -> x0, loops' own time: 2.88 us -> none  [the longest x1 2.74 us: body(): lax.fori_loop(0, turns, one_block, jnp.zeros((slots, K), jnp.float32))]
  transfers between devices with their start and end apart: 1 -> 0, of which waited for: 1 -> 0; matrix products, arithmetic and copies ran while one was open for 10% -> 0% of each run, Pallas kernels for 0% -> 0%
where the time goes in v1:
time: 32.9 us; the launch traced here: 32.6 us
  Pallas kernels  25.2 us (77%)
  local copies, waits for them, and re-layouts  6.12 us (19%)
  between operations  1.3 us (4%)
    pallas_call x1, Pallas kernels, body(): pl.pallas_call(functools.partial(kernel, n, chunk), out_shape=(jax.ShapeD...  25.2 us
    unnamed x12, local copies, waits for them, and re-layouts  6.12 us

profile of v1, /device:TPU:0, one launch (start us, length us, event | category | flops | bytes accessed | tf_op | source)
XLA Modules:
  0.0 32.6 jit_solution(3408039607906843788)
XLA Ops:
  1.3 0.0 copy-start
  1.3 2.2 %copy-done = bf16[1024,2048]{1,0:T(8,128)(2,1)S(1)} copy-done((bf16[1024,2048]{1,0:T(8,128)(2,1)S(1)}, bf16[1024,2048]{1,0:T(8,128)(2,1)}, u32[]{:S(2)}) %copy-start) | copy-done | bytes 4194328
  3.5 0.0 copy-start.1
  3.5 0.7 %copy-done.1 = f32[1024]{0:T(1024)S(1)} copy-done((f32[1024]{0:T(1024)S(1)}, f32[1024]{0:T(1024)}, u32[]{:S(2)}) %copy-start.1) | copy-done | bytes 4120
  4.2 0.0 copy-start.2
  4.2 0.7 %copy-done.2 = f32[1024]{0:T(1024)S(1)} copy-done((f32[1024]{0:T(1024)S(1)}, f32[1024]{0:T(1024)}, u32[]{:S(2)}) %copy-start.2) | copy-done | bytes 4120
  4.8 0.0 copy-start.3
  4.8 0.7 %copy-done.3 = s32[1024]{0:T(1024)S(1)} copy-done((s32[1024]{0:T(1024)S(1)}, s32[1024]{0:T(1024)}, u32[]{:S(2)}) %copy-start.3) | copy-done | bytes 4120
  5.5 0.0 copy-start.4
  5.5 0.7 %copy-done.4 = s32[64]{0:T(128)S(1)} copy-done((s32[64]{0:T(128)S(1)}, s32[64]{0:T(128)}, u32[]{:S(2)}) %copy-start.4) | copy-done | bytes 280
  6.2 25.2 %shard_map.86 = (f32[1,256]{1,0:T(1,128)S(1)}, f32[64,8]{1,0:T(8,128)S(1)}) custom-call(s32[64]{0:T(128)S(1)} %copy-done.4, s32[1]{0:T(128)S(6)} %copy.11.count_ref, bf16[1024,2048]{1,0:T(8,128)(2,1)S(1)} %copy-done, bf16[2048,1024]{1,0:T(8,128)(2,1)} %sens_hbm.1, f32[1,1024]{1,0:T(1,128)S(1)} %bitcast.4, f32[1,1024]{1,0:T(1,128)S(1)} %bitcast.5, ...), custom_call_target="tpu_custom_call" | custom-call | tf_op jit(solution)/shard_map/pallas_call | solution.py:252
  31.4 0.7 %copy.9 = f32[64,8]{0,1:T(8,128)} copy(f32[64,8]{1,0:T(8,128)S(1)} %get-tuple-element.7) | data formatting | bytes 4096
  32.1 0.6 %copy.12 = f32[256]{0:T(256)} copy(f32[256]{0:T(256)S(1)} %bitcast.7) | data formatting | bytes 2048
Async XLA Ops:
  1.3 2.2 %copy-start = (bf16[1024,2048]{1,0:T(8,128)(2,1)S(1)}, bf16[1024,2048]{1,0:T(8,128)(2,1)}, u32[]{:S(2)}) copy-start(bf16[1024,2048]{1,0:T(8,128)(2,1)} %shocks_hbm.1) | copy-start | bytes 12582916
  3.5 0.7 %copy-start.1 = (f32[1024]{0:T(1024)S(1)}, f32[1024]{0:T(1024)}, u32[]{:S(2)}) copy-start(f32[1024]{0:T(1024)} %param.9) | copy-start | bytes 12292
  4.2 0.7 %copy-start.2 = (f32[1024]{0:T(1024)S(1)}, f32[1024]{0:T(1024)}, u32[]{:S(2)}) copy-start(f32[1024]{0:T(1024)} %param.10) | copy-start | bytes 12292
  4.8 0.7 %copy-start.3 = (s32[1024]{0:T(1024)S(1)}, s32[1024]{0:T(1024)}, u32[]{:S(2)}) copy-start(s32[1024]{0:T(1024)} %param.13) | copy-start | bytes 12292
  5.5 0.7 %copy-start.4 = (s32[64]{0:T(128)S(1)}, s32[64]{0:T(128)}, u32[]{:S(2)}) copy-start(s32[64]{0:T(128)} %ent_ref.1) | copy-start | bytes 772

commit v2 on v1

v2 whole, which is shorter than its diff:
```python
import functools

import jax
import jax.numpy as jnp
from jax import lax
from jax.experimental import pallas as pl
from jax.experimental.pallas import tpu as pltpu
from jax.sharding import PartitionSpec as P

INSTR = 16
ENT = 8
TOPK = 256
LANES = 128
LOW = -1e30


def bitonic_sort(x, ascending):
    lane = lax.broadcasted_iota(jnp.int32, (x.shape[0], LANES), 1)
    parts = [x[:, p * LANES : (p + 1) * LANES] for p in range(TOPK // LANES)]
    a, b = parts
    big, small = jnp.maximum(a, b), jnp.minimum(a, b)
    parts = [jnp.where(ascending, small, big), jnp.where(ascending, big, small)]
    step = LANES // 2
    while step:
        first = (lane & step) == 0
        keep_big = first != ascending
        out = []
        for p in parts:
            other = jnp.where(first, pltpu.roll(p, LANES - step, 1), pltpu.roll(p, step, 1))
            out.append(jnp.where(keep_big, jnp.maximum(p, other), jnp.minimum(p, other)))
        parts = out
        step //= 2
    return jnp.concatenate(parts, axis=1)


def kernel(
    n,
    chunk,
    count_ref,
    ent_hbm,
    shocks_hbm,
    sens_hbm,
    notional_hbm,
    money_hbm,
    ids_hbm,
    tail_ref,
    cand_ref,
    ent_ref,
    notional_ref,
    money_ref,
    ids_ref,
    base_ref,
    shocks,
    sens,
    value_a,
    value_b,
    weight,
    sums,
    row_loss,
    col_loss,
    tail_send,
    tail_recv,
    cand_send,
    cand_recv,
    merged,
    x_sem,
    w_sem,
    small_sem,
    tail_ssem,
    tail_rsem,
    cand_ssem,
    cand_rsem,
):
    slots, factors = shocks.shape
    quarters, _, width = sens.shape
    cols = quarters * width
    rows = value_a.shape[0]
    steps = (slots // rows) * quarters
    me = lax.axis_index("scen")

    def w_copy(q):
        return pltpu.make_async_copy(sens_hbm.at[:, pl.ds(q * width, width)], sens.at[q], w_sem.at[q])

    def x_copy(h):
        return pltpu.make_async_copy(
            shocks_hbm.at[pl.ds(h * rows, rows), :], shocks.at[pl.ds(h * rows, rows), :], x_sem.at[h]
        )

    small = [pltpu.make_async_copy(ent_hbm, ent_ref, small_sem.at[0])]
    for q in range(quarters):
        part = pl.ds(q * width, width)
        small.append(pltpu.make_async_copy(notional_hbm.at[:, part], notional_ref.at[q], small_sem.at[1 + 2 * q]))
        small.append(pltpu.make_async_copy(money_hbm.at[:, part], money_ref.at[q], small_sem.at[2 + 2 * q]))
    ids_copy = pltpu.make_async_copy(ids_hbm, ids_ref, small_sem.at[1 + 2 * quarters])
    for c in small:
        c.start()
    w_copy(0).start()
    x_copy(0).start()
    for q in range(1, quarters):
        w_copy(q).start()
    for h in range(1, slots // rows):
        x_copy(h).start()
    ids_copy.start()

    barrier = pltpu.get_barrier_semaphore()
    for k in range(1, n):
        pl.semaphore_signal(barrier, inc=1, device_id={"scen": lax.rem(me + k, n)}, device_id_type=pl.DeviceIdType.MESH)

    for c in small:
        c.wait()
    wlane = lax.broadcasted_iota(jnp.int32, (INSTR, 2 * LANES), 1)
    for k in range(cols // INSTR):
        hit = (wlane == ent_ref[k]) | (wlane >= LANES)
        weight[k * INSTR : (k + 1) * INSTR, :] = jnp.where(hit, -1.0, 0.0).astype(jnp.bfloat16)
    money = money_ref[...]
    base_ref[...] = jnp.maximum(money, 0.0) + jnp.log(1.0 + jnp.exp(-jnp.abs(money)))
    sums[...] = jnp.zeros_like(sums)

    def matmul(s, value):
        h, q = lax.div(s, quarters), lax.rem(s, quarters)
        x = shocks[pl.ds(pl.multiple_of(h * rows, rows), rows), :]
        value[...] = jnp.dot(x, sens[q], preferred_element_type=jnp.float32)

    def finish(s, value):
        h, q = lax.div(s, quarters), lax.rem(s, quarters)
        z = value[...] + money_ref[q]
        inst = notional_ref[q] * (jnp.maximum(z, 0.0) + jnp.log(1.0 + jnp.exp(-jnp.abs(z))) - base_ref[q])
        hi = inst.astype(jnp.bfloat16)
        lo = (inst - hi.astype(jnp.float32)).astype(jnp.bfloat16)
        w = weight[pl.ds(pl.multiple_of(q * width, width), width), :]
        total = jnp.dot(hi, w, preferred_element_type=jnp.float32) + jnp.dot(lo, w, preferred_element_type=jnp.float32)
        sums[pl.ds(pl.multiple_of(h * rows, rows), rows), :] += total

    def arrive(s):
        for q in range(1, quarters):
            @pl.when(s == q)
            def _():
                w_copy(q).wait()
        for h in range(1, slots // rows):
            @pl.when(s == h * quarters)
            def _():
                x_copy(h).wait()

    w_copy(0).wait()
    x_copy(0).wait()
    matmul(0, value_a)

    def pair(j, unused):
        arrive(2 * j + 1)
        arrive(2 * j + 2)
        matmul(2 * j + 1, value_b)
        finish(2 * j, value_a)
        matmul(2 * j + 2, value_a)
        finish(2 * j + 1, value_b)
        return unused

    lax.fori_loop(0, steps // 2 - 1, pair, 0)
    arrive(jnp.int32(steps - 1))
    matmul(steps - 1, value_b)
    finish(steps - 2, value_a)
    finish(steps - 1, value_b)

    def cand_copy(k):
        peer = lax.rem(me + k, n)
        return pltpu.make_async_remote_copy(
            src_ref=cand_send.at[peer],
            dst_ref=cand_recv.at[me],
            send_sem=cand_ssem.at[k],
            recv_sem=cand_rsem.at[k],
            device_id={"scen": peer},
            device_id_type=pl.DeviceIdType.MESH,
        )

    entity = jnp.concatenate(
        [sums[t * LANES : (t + 1) * LANES, :LANES].T[:ENT, :] for t in range(slots // LANES)], axis=1
    )
    hi = entity.astype(jnp.bfloat16).astype(jnp.float32)
    rest = entity - hi
    mid = rest.astype(jnp.bfloat16).astype(jnp.float32)
    split = jnp.concatenate([hi, mid, rest - mid], axis=0).astype(jnp.bfloat16)
    ids_copy.wait()
    packed = cand_send.shape[1]
    lane = lax.broadcasted_iota(jnp.int32, (packed, LANES), 1)
    span = 2 * LANES
    for p in range(ids_ref.shape[1] // span):
        local = ids_ref[:, p * span : (p + 1) * span] - me * slots
        hot = lax.broadcasted_iota(jnp.int32, (slots, span), 0) == local
        hot = jnp.where(hot, 1.0, 0.0).astype(jnp.bfloat16)
        got = jnp.dot(split, hot, preferred_element_type=jnp.float32)
        got = got[:ENT] + got[ENT : 2 * ENT] + got[2 * ENT :]
        for d in range(span // chunk):
            first = d * chunk // LANES * LANES
            offset = d * chunk - first
            message = None
            for j in range(ENT // packed):
                piece = got[j * packed : (j + 1) * packed, first : first + LANES]
                shift = (j * chunk - offset) % LANES
                if shift:
                    piece = pltpu.roll(piece, shift, 1)
                message = piece if message is None else jnp.where(lane >= j * chunk, piece, message)
            cand_send[p * (span // chunk) + d] = message
    cand_recv[me] = cand_send[me]

    pl.semaphore_wait(barrier, n - 1)
    for k in range(1, n):
        cand_copy(k).start()

    count = count_ref[0]
    sub = lax.broadcasted_iota(jnp.int32, (LANES, LANES), 0)
    for t in range(slots // LANES):
        loss = sums[t * LANES : (t + 1) * LANES, LANES:]
        loss = jnp.where(sub + t * LANES < count, loss, LOW)
        col_loss[t * LANES : (t + 1) * LANES, :] = loss
        row_loss[:, t * LANES : (t + 1) * LANES] = loss.T[:8, :]
    rank = lax.broadcasted_iota(jnp.int32, (LANES, LANES), 1)
    order = lax.select(me >= n // 2, 1, 0)
    rank_lo = (rank + order * (TOPK - 1 - 2 * rank)).astype(jnp.float32)
    rank_hi = (rank + LANES + order * (TOPK - 1 - 2 * (rank + LANES))).astype(jnp.float32)
    ones = jnp.ones((LANES, LANES), jnp.bfloat16)

    def ranked(t, best):
        mine = col_loss[pl.ds(pl.multiple_of(t * LANES, LANES), LANES), :]
        larger = jnp.zeros((LANES, LANES), jnp.float32)
        for s in range(slots // LANES):
            theirs = row_loss[0:1, s * LANES : (s + 1) * LANES]
            larger = larger + jnp.where(theirs > mine, 1.0, 0.0)
        place = jnp.dot(larger.astype(jnp.bfloat16), ones, preferred_element_type=jnp.float32)
        b_lo, b_hi = best
        b_lo = jnp.minimum(b_lo, jnp.min(jnp.where(place <= rank_lo, mine, jnp.inf), axis=0, keepdims=True))
        b_hi = jnp.minimum(b_hi, jnp.min(jnp.where(place <= rank_hi, mine, jnp.inf), axis=0, keepdims=True))
        return b_lo, b_hi

    empty = jnp.full((1, LANES), jnp.inf, jnp.float32)
    b_lo, b_hi = lax.fori_loop(0, slots // LANES, ranked, (empty, empty))
    top = jnp.concatenate([b_lo, b_hi], axis=1)
    tail_send[...] = top
    tail_recv[me] = top

    def tail_copy(k):
        return pltpu.make_async_remote_copy(
            src_ref=tail_send,
            dst_ref=tail_recv.at[me],
            send_sem=tail_ssem.at[k],
            recv_sem=tail_rsem.at[k],
            device_id={"scen": lax.rem(me + k, n)},
            device_id_type=pl.DeviceIdType.MESH,
        )

    for k in range(1, n):
        tail_copy(k).start()

    for k in range(1, n):
        tail_copy(k).wait_recv()
    for b in range(n):
        merged[b : b + 1, :] = tail_recv[b]
    lists = n
    while lists > 1:
        half = lists // 2
        if lists == n:
            x = merged[...]
        x = jnp.maximum(x[:half], x[half : 2 * half])
        pad = max(half, 8)
        if half < 8:
            x = jnp.concatenate([x] * (pad // half), axis=0)
        row = lax.broadcasted_iota(jnp.int32, (pad, LANES), 0)
        ascending = row >= (half // 2 if half > 1 else pad)
        x = bitonic_sort(x, ascending)
        lists = half
    tail_ref[...] = x[:1, :]

    for k in range(1, n):
        cand_copy(k).wait_recv()
    total = cand_recv[0]
    for b in range(1, n):
        total = total + cand_recv[b]
    cand_ref[...] = jnp.concatenate([total[:, j * chunk : (j + 1) * chunk] for j in range(ENT // packed)], axis=0)
    for k in range(1, n):
        tail_copy(k).wait_send()
        cand_copy(k).wait_send()


def deliver(tail_in, cand_in, tail_out, cand_out):
    tail_out[...] = tail_in[...]
    cand_out[...] = cand_in[...]


def body(n, shocks, factor_sens, notional, moneyness, desk_entity, scenario_counts, candidate_ids):
    slots, factors = shocks.shape
    cols = factor_sens.shape[1]
    cands = candidate_ids.shape[0]
    chunk = cands // n
    packed = ENT // min(ENT, LANES // chunk)
    width = cols // 4
    rows = slots // 2
    vmem = pl.BlockSpec(memory_space=pltpu.VMEM)
    smem = pl.BlockSpec(memory_space=pltpu.SMEM)
    hbm = pl.BlockSpec(memory_space=pltpu.HBM)
    shapes = (
        jax.ShapeDtypeStruct((1, TOPK), jnp.float32),
        jax.ShapeDtypeStruct((ENT, chunk), jnp.float32),
    )
    tail, cand = pl.pallas_call(
        functools.partial(kernel, n, chunk),
        out_shape=shapes,
        in_specs=[smem, hbm, hbm, hbm, hbm, hbm, hbm],
        out_specs=(vmem, vmem),
        scratch_shapes=[
            pltpu.SMEM(desk_entity.shape, jnp.int32),
            pltpu.VMEM((4, 1, width), jnp.float32),
            pltpu.VMEM((4, 1, width), jnp.float32),
            pltpu.VMEM((1, cands), jnp.int32),
            pltpu.VMEM((4, 1, width), jnp.float32),
            pltpu.VMEM((slots, factors), jnp.bfloat16),
            pltpu.VMEM((4, factors, width), jnp.bfloat16),
            pltpu.VMEM((rows, width), jnp.float32),
            pltpu.VMEM((rows, width), jnp.float32),
            pltpu.VMEM((cols, 2 * LANES), jnp.bfloat16),
            pltpu.VMEM((slots, 2 * LANES), jnp.float32),
            pltpu.VMEM((8, slots), jnp.float32),
            pltpu.VMEM((slots, LANES), jnp.float32),
            pltpu.VMEM((1, TOPK), jnp.float32),
            pltpu.VMEM((n, 1, TOPK), jnp.float32),
            pltpu.VMEM((n, packed, LANES), jnp.float32),
            pltpu.VMEM((n, packed, LANES), jnp.float32),
            pltpu.VMEM((n, TOPK), jnp.float32),
            pltpu.SemaphoreType.DMA((2,)),
            pltpu.SemaphoreType.DMA((4,)),
            pltpu.SemaphoreType.DMA((10,)),
            pltpu.SemaphoreType.DMA((n,)),
            pltpu.SemaphoreType.DMA((n,)),
            pltpu.SemaphoreType.DMA((n,)),
            pltpu.SemaphoreType.DMA((n,)),
        ],
        compiler_params=pltpu.CompilerParams(
            collective_id=0, has_side_effects=True, vmem_limit_bytes=67043328
        ),
    )(
        scenario_counts,
        desk_entity,
        shocks,
        factor_sens,
        notional.reshape(1, cols),
        moneyness.reshape(1, cols),
        candidate_ids.reshape(1, cands),
    )
    tail, cand = pl.pallas_call(deliver, out_shape=shapes, in_specs=[vmem, vmem], out_specs=(vmem, vmem))(tail, cand)
    return tail.reshape(TOPK), cand.T


def solution(mesh):
    return jax.shard_map(
        functools.partial(body, mesh.shape["scen"]),
        mesh=mesh,
        in_specs=(P(("grp", "scen"), None), P(), P(), P(), P(), P(("grp", "scen")), P("grp")),
        out_specs=(P("grp"), P(("grp", "scen"), None)),
        check_vma=False,
    )
```

time: 32.9 us -> 26.3 us (0.80)
  local copies, waits for them, and re-layouts: 6.12 us -> 0 us
    unnamed x12 -> x0, local copies, waits for them, and re-layouts: 6.12 us -> none
    pallas_call x1 -> x2, Pallas kernels: 25.2 us -> 24.9 us  [the longest x1 23.6 us: body(): pl.pallas_call(functools.partial(kernel, n, chunk), out_shape=shapes, in_...]
where the time goes in v2:
time: 26.3 us; the launch traced here: 26.1 us
  Pallas kernels  24.9 us (95%)
  between operations  1.29 us (5%)
    pallas_call x1, Pallas kernels, body(): pl.pallas_call(functools.partial(kernel, n, chunk), out_shape=shapes, in_...  23.6 us
    pallas_call x1, Pallas kernels, body(): pl.pallas_call(deliver, out_shape=shapes, in_specs=[vmem, vmem], out_spec...  1.27 us

profile of v2, /device:TPU:0, one launch (start us, length us, event | category | flops | bytes accessed | tf_op | source)
XLA Modules:
  0.0 26.1 jit_solution(6854994728326422508)
XLA Ops:
  1.3 23.6 %shard_map.86 = (f32[1,256]{1,0:T(1,128)}, f32[8,64]{1,0:T(8,128)}) custom-call(s32[1]{0:T(128)S(6)} %copy.9.count_ref, s32[64]{0:T(128)} %ent_hbm.1, bf16[1024,2048]{1,0:T(8,128)(2,1)} %shocks_hbm.1, bf16[2048,1024]{1,0:T(8,128)(2,1)} %sens_hbm.1, f32[1,1024]{1,0:T(1,128)} %bitcast.5, f32[1,1024]{1,0:T(1,128)} %bitcast.6, s32[1,1024]{1,0:T(1,128)} %bitcast.7), custom_call_target="tpu_custom_call" | custom-call | tf_op jit(solution)/shard_map/pallas_call | solution.py:302
  24.9 1.3 %shard_map.87 = (f32[1,256]{1,0:T(1,128)}, f32[8,64]{1,0:T(8,128)}) custom-call(f32[1,256]{1,0:T(1,128)} %get-tuple-element.6.tail_in, f32[8,64]{1,0:T(8,128)} %get-tuple-element.7.cand_in), custom_call_target="tpu_custom_call" | custom-call | tf_op jit(solution)/shard_map/pallas_call | solution.py:346

commit v3 on v2

v3 whole, which is shorter than its diff:
```python
import functools

import jax
import jax.numpy as jnp
from jax import lax
from jax.experimental import pallas as pl
from jax.experimental.pallas import tpu as pltpu
from jax.sharding import PartitionSpec as P

INSTR = 16
ENT = 8
TOPK = 256
LANES = 128
LOW = -1e30


def bitonic_sort(x, ascending):
    lane = lax.broadcasted_iota(jnp.int32, (x.shape[0], LANES), 1)
    parts = [x[:, p * LANES : (p + 1) * LANES] for p in range(TOPK // LANES)]
    a, b = parts
    big, small = jnp.maximum(a, b), jnp.minimum(a, b)
    parts = [jnp.where(ascending, small, big), jnp.where(ascending, big, small)]
    step = LANES // 2
    while step:
        first = (lane & step) == 0
        keep_big = first != ascending
        out = []
        for p in parts:
            other = jnp.where(first, pltpu.roll(p, LANES - step, 1), pltpu.roll(p, step, 1))
            out.append(jnp.where(keep_big, jnp.maximum(p, other), jnp.minimum(p, other)))
        parts = out
        step //= 2
    return jnp.concatenate(parts, axis=1)


def kernel(
    n,
    chunk,
    count_ref,
    ent_hbm,
    shocks_hbm,
    sens_hbm,
    notional_hbm,
    money_hbm,
    ids_hbm,
    tail_ref,
    cand_ref,
    ent_ref,
    notional_ref,
    money_ref,
    ids_ref,
    base_ref,
    shocks,
    sens,
    value,
    weight,
    sums,
    entity,
    row_loss,
    col_loss,
    send,
    recv,
    merged,
    x_sem,
    w_sem,
    small_sem,
    send_sem,
    recv_sem,
):
    slots, factors = shocks.shape
    quarters, _, width = sens.shape
    cols = quarters * width
    rows = value.shape[0]
    groups = slots // rows
    half = groups // 2 * quarters
    steps = groups * quarters
    packed = send.shape[1] - TOPK // LANES
    me = lax.axis_index("scen")

    def w_copy(q):
        return pltpu.make_async_copy(
            sens_hbm.at[:, pl.ds(pl.multiple_of(q * width, width), width)], sens.at[q], w_sem.at[q]
        )

    def x_copy(h):
        part = pl.ds(pl.multiple_of(h * (slots // 2), slots // 2), slots // 2)
        return pltpu.make_async_copy(shocks_hbm.at[part, :], shocks.at[part, :], x_sem.at[h])

    small = [pltpu.make_async_copy(ent_hbm, ent_ref, small_sem.at[0])]
    for q in range(quarters):
        part = pl.ds(q * width, width)
        small.append(pltpu.make_async_copy(notional_hbm.at[:, part], notional_ref.at[q], small_sem.at[1 + 2 * q]))
        small.append(pltpu.make_async_copy(money_hbm.at[:, part], money_ref.at[q], small_sem.at[2 + 2 * q]))
    w_copy(0).start()
    x_copy(0).start()
    for c in small:
        c.start()
    for q in range(1, quarters):
        w_copy(q).start()
    x_copy(1).start()
    spans = ids_ref.shape[0]
    span = ids_ref.shape[2]
    ids_copies = [
        pltpu.make_async_copy(ids_hbm.at[:, pl.ds(p * span, span)], ids_ref.at[p], small_sem.at[1 + 2 * quarters + p])
        for p in range(spans)
    ]
    for c in ids_copies:
        c.start()

    barrier = pltpu.get_barrier_semaphore()

    def greet(k, unused):
        pl.semaphore_signal(
            barrier, inc=1, device_id={"scen": lax.rem(me + k, n)}, device_id_type=pl.DeviceIdType.MESH
        )
        return unused

    lax.fori_loop(1, n, greet, 0)

    for c in small:
        c.wait()
    wlane = lax.broadcasted_iota(jnp.int32, (INSTR, 2 * LANES), 1)

    def spread(k, unused):
        hit = (wlane == ent_ref[k]) | (wlane >= LANES)
        part = pl.ds(pl.multiple_of(k * INSTR, INSTR), INSTR)
        weight[part, :] = jnp.where(hit, -1.0, 0.0).astype(jnp.bfloat16)
        return unused

    lax.fori_loop(0, cols // INSTR, spread, 0)
    money = money_ref[...]
    base_ref[...] = jnp.maximum(money, 0.0) + jnp.log(1.0 + jnp.exp(-jnp.abs(money)))
    notional_ref[quarters] = jnp.zeros((1, width), jnp.float32)

    def clear(t, unused):
        part = pl.ds(pl.multiple_of(t * LANES, LANES), LANES)
        sums[part, :] = jnp.zeros((LANES, 2 * LANES), jnp.float32)
        return unused

    lax.fori_loop(0, slots // LANES, clear, 0)

    def clear_value(t, unused):
        part = pl.ds(pl.multiple_of(t * 64, 64), 64)
        value[part, :] = jnp.zeros((64, width), jnp.float32)
        return unused

    lax.fori_loop(0, rows // 64, clear_value, 0)

    def place(s):
        h = lax.div(s, half)
        q = lax.div(lax.rem(s, half), groups // 2)
        g = lax.rem(s, groups // 2)
        return q, pl.ds(pl.multiple_of((h * (groups // 2) + g) * rows, rows), rows)

    def step(s, unused):
        for q in range(quarters):
            @pl.when(s == q * (groups // 2))
            def _():
                w_copy(q).wait()
                if q == 0:
                    x_copy(0).wait()

        @pl.when(s == half)
        def _():
            x_copy(1).wait()

        q, part = place(lax.rem(s + steps - 1, steps))
        z = value[...] + money_ref[q]
        scale = notional_ref[lax.select(s == 0, quarters, q)]
        inst = scale * (jnp.maximum(z, 0.0) + jnp.log(1.0 + jnp.exp(-jnp.abs(z))) - base_ref[q])
        hi = inst.astype(jnp.bfloat16)
        lo = (inst - hi.astype(jnp.float32)).astype(jnp.bfloat16)
        w = weight[pl.ds(pl.multiple_of(q * width, width), width), :]
        total = jnp.dot(hi, w, preferred_element_type=jnp.float32) + jnp.dot(lo, w, preferred_element_type=jnp.float32)
        sums[part, :] += total
        q, part = place(lax.rem(s, steps))
        value[...] = jnp.dot(shocks[part, :], sens[q], preferred_element_type=jnp.float32)
        return unused

    lax.fori_loop(0, steps + 1, step, 0)

    count = count_ref[0]
    sub = lax.broadcasted_iota(jnp.int32, (LANES, LANES), 0)
    for c in ids_copies:
        c.wait()

    def arrange(t, unused):
        part = pl.ds(pl.multiple_of(t * LANES, LANES), LANES)
        loss = jnp.where(sub + t * LANES < count, sums[part, LANES:], LOW)
        col_loss[part, :] = loss
        row_loss[t] = loss.T[:8, :]
        sides = sums[part, :LANES].T[:ENT, :]
        hi = sides.astype(jnp.bfloat16).astype(jnp.float32)
        rest = sides - hi
        mid = rest.astype(jnp.bfloat16).astype(jnp.float32)
        entity[t] = jnp.concatenate([hi, mid, rest - mid, jnp.zeros_like(hi)], axis=0).astype(jnp.bfloat16)
        return unused

    lax.fori_loop(0, slots // LANES, arrange, 0)
    split = jnp.concatenate([entity[t] for t in range(slots // LANES)], axis=1)
    lane = lax.broadcasted_iota(jnp.int32, (packed, LANES), 1)

    def select(p, unused):
        local = ids_ref[p] - me * slots
        hot = lax.broadcasted_iota(jnp.int32, (slots, span), 0) == local
        hot = jnp.where(hot, 1.0, 0.0).astype(jnp.bfloat16)
        got = jnp.dot(split, hot, preferred_element_type=jnp.float32)
        got = got[:ENT] + got[ENT : 2 * ENT] + got[2 * ENT : 3 * ENT]
        for d in range(span // chunk):
            first = d * chunk // LANES * LANES
            offset = d * chunk - first
            message = None
            for j in range(ENT // packed):
                piece = got[j * packed : (j + 1) * packed, first : first + LANES]
                shift = (j * chunk - offset) % LANES
                if shift:
                    piece = pltpu.roll(piece, shift, 1)
                message = piece if message is None else jnp.where(lane >= j * chunk, piece, message)
            send[p * (span // chunk) + d, :packed, :] = message
        return unused

    lax.fori_loop(0, spans, select, 0)

    rank = lax.broadcasted_iota(jnp.int32, (LANES, LANES), 1)
    order = lax.select(me >= n // 2, 1, 0)
    rank_lo = (rank + order * (TOPK - 1 - 2 * rank)).astype(jnp.float32)
    rank_hi = (rank + LANES + order * (TOPK - 1 - 2 * (rank + LANES))).astype(jnp.float32)
    ones = jnp.ones((LANES, LANES), jnp.bfloat16)

    def ranked(t, best):
        mine = col_loss[pl.ds(pl.multiple_of(t * LANES, LANES), LANES), :]
        larger = jnp.zeros((LANES, LANES), jnp.float32)
        for s in range(slots // LANES):
            larger = larger + jnp.where(row_loss[s][:1, :] > mine, 1.0, 0.0)
        above = jnp.dot(larger.astype(jnp.bfloat16), ones, preferred_element_type=jnp.float32)
        b_lo, b_hi = best
        b_lo = jnp.minimum(b_lo, jnp.min(jnp.where(above <= rank_lo, mine, jnp.inf), axis=0, keepdims=True))
        b_hi = jnp.minimum(b_hi, jnp.min(jnp.where(above <= rank_hi, mine, jnp.inf), axis=0, keepdims=True))
        return b_lo, b_hi

    empty = jnp.full((1, LANES), jnp.inf, jnp.float32)
    b_lo, b_hi = lax.fori_loop(0, slots // LANES, ranked, (empty, empty))

    def attach(d, unused):
        send[d, packed : packed + 1, :] = b_lo
        send[d, packed + 1 :, :] = b_hi
        return unused

    lax.fori_loop(0, n, attach, 0)
    recv[me] = send[me]

    def message_copy(k):
        peer = lax.rem(me + k, n)
        return pltpu.make_async_remote_copy(
            src_ref=send.at[peer],
            dst_ref=recv.at[me],
            send_sem=send_sem.at[k],
            recv_sem=recv_sem.at[k],
            device_id={"scen": peer},
            device_id_type=pl.DeviceIdType.MESH,
        )

    pl.semaphore_wait(barrier, n - 1)

    def start(k, unused):
        message_copy(k).start()
        return unused

    def arrived(k, unused):
        message_copy(k).wait_recv()
        return unused

    def sent(k, unused):
        message_copy(k).wait_send()
        return unused

    lax.fori_loop(1, n, start, 0)
    lax.fori_loop(1, n, arrived, 0)

    total = jnp.zeros((packed, LANES), jnp.float32)
    for b in range(n):
        total = total + recv[b, :packed, :]
        merged[b : b + 1, :LANES] = recv[b, packed : packed + 1, :]
        merged[b : b + 1, LANES:] = recv[b, packed + 1 :, :]
    cand_ref[...] = jnp.concatenate([total[:, j * chunk : (j + 1) * chunk] for j in range(ENT // packed)], axis=0)
    x = merged[...]
    lists = n
    while lists > 1:
        keep = lists // 2
        x = jnp.maximum(x[:keep], x[keep : 2 * keep])
        pad = max(keep, 8)
        if keep < 8:
            x = jnp.concatenate([x] * (pad // keep), axis=0)
        row = lax.broadcasted_iota(jnp.int32, (pad, LANES), 0)
        x = bitonic_sort(x, row >= (keep // 2 if keep > 1 else pad))
        lists = keep
    tail_ref[...] = x[:1, :]
    lax.fori_loop(1, n, sent, 0)


def deliver(tail_in, cand_in, tail_out, cand_out):
    tail_out[...] = tail_in[...]
    cand_out[...] = cand_in[...]


def body(n, shocks, factor_sens, notional, moneyness, desk_entity, scenario_counts, candidate_ids):
    slots, factors = shocks.shape
    cols = factor_sens.shape[1]
    cands = candidate_ids.shape[0]
    chunk = cands // n
    packed = ENT // min(ENT, LANES // chunk)
    width = cols // 4
    rows = slots // 4
    span = 2 * LANES
    vmem = pl.BlockSpec(memory_space=pltpu.VMEM)
    smem = pl.BlockSpec(memory_space=pltpu.SMEM)
    hbm = pl.BlockSpec(memory_space=pltpu.HBM)
    shapes = (
        jax.ShapeDtypeStruct((1, TOPK), jnp.float32),
        jax.ShapeDtypeStruct((ENT, chunk), jnp.float32),
    )
    tail, cand = pl.pallas_call(
        functools.partial(kernel, n, chunk),
        out_shape=shapes,
        in_specs=[smem, hbm, hbm, hbm, hbm, hbm, hbm],
        out_specs=(vmem, vmem),
        scratch_shapes=[
            pltpu.SMEM(desk_entity.shape, jnp.int32),
            pltpu.VMEM((5, 1, width), jnp.float32),
            pltpu.VMEM((4, 1, width), jnp.float32),
            pltpu.VMEM((cands // span, 1, span), jnp.int32),
            pltpu.VMEM((4, 1, width), jnp.float32),
            pltpu.VMEM((slots, factors), jnp.bfloat16),
            pltpu.VMEM((4, factors, width), jnp.bfloat16),
            pltpu.VMEM((rows, width), jnp.float32),
            pltpu.VMEM((cols, 2 * LANES), jnp.bfloat16),
            pltpu.VMEM((slots, 2 * LANES), jnp.float32),
            pltpu.VMEM((slots // LANES, 4 * ENT, LANES), jnp.bfloat16),
            pltpu.VMEM((slots // LANES, 8, LANES), jnp.float32),
            pltpu.VMEM((slots, LANES), jnp.float32),
            pltpu.VMEM((n, packed + TOPK // LANES, LANES), jnp.float32),
            pltpu.VMEM((n, packed + TOPK // LANES, LANES), jnp.float32),
            pltpu.VMEM((n, TOPK), jnp.float32),
            pltpu.SemaphoreType.DMA((2,)),
            pltpu.SemaphoreType.DMA((4,)),
            pltpu.SemaphoreType.DMA((9 + cands // span,)),
            pltpu.SemaphoreType.DMA((n,)),
            pltpu.SemaphoreType.DMA((n,)),
        ],
        compiler_params=pltpu.CompilerParams(
            collective_id=0, has_side_effects=True, vmem_limit_bytes=67043328
        ),
    )(
        scenario_counts,
        desk_entity,
        shocks,
        factor_sens,
        notional.reshape(1, cols),
        moneyness.reshape(1, cols),
        candidate_ids.reshape(1, cands),
    )
    tail, cand = pl.pallas_call(deliver, out_shape=shapes, in_specs=[vmem, vmem], out_specs=(vmem, vmem))(tail, cand)
    return tail.reshape(TOPK), cand.T


def solution(mesh):
    return jax.shard_map(
        functools.partial(body, mesh.shape["scen"]),
        mesh=mesh,
        in_specs=(P(("grp", "scen"), None), P(), P(), P(), P(), P(("grp", "scen")), P("grp")),
        out_specs=(P("grp"), P(("grp", "scen"), None)),
        check_vma=False,
    )
```

time: 26.3 us -> 28.8 us (1.095)
  Pallas kernels: 24.9 us -> 27.4 us
    pallas_call x1, Pallas kernels: 23.6 us -> 26.1 us  [body(): pl.pallas_call(functools.partial(kernel, n, chunk), out_shape=shapes, in_...]
where the time goes in v3:
time: 28.8 us; the launch traced here: 28.7 us
  Pallas kernels  27.4 us (95%)
  between operations  1.29 us (4%)
    pallas_call x1, Pallas kernels, body(): pl.pallas_call(functools.partial(kernel, n, chunk), out_shape=shapes, in_...  26.1 us
    pallas_call x1, Pallas kernels, body(): pl.pallas_call(deliver, out_shape=shapes, in_specs=[vmem, vmem], out_spec...  1.27 us

profile of v3, /device:TPU:0, one launch (start us, length us, event | category | flops | bytes accessed | tf_op | source)
XLA Modules:
  0.0 28.7 jit_solution(3201441180433184655)
XLA Ops:
  1.3 26.1 %shard_map.86 = (f32[1,256]{1,0:T(1,128)}, f32[8,64]{1,0:T(8,128)}) custom-call(s32[1]{0:T(128)S(6)} %copy.9.count_ref, s32[64]{0:T(128)} %ent_hbm.1, bf16[1024,2048]{1,0:T(8,128)(2,1)} %shocks_hbm.1, bf16[2048,1024]{1,0:T(8,128)(2,1)} %sens_hbm.1, f32[1,1024]{1,0:T(1,128)} %bitcast.5, f32[1,1024]{1,0:T(1,128)} %bitcast.6, s32[1,1024]{1,0:T(1,128)} %bitcast.7), custom_call_target="tpu_custom_call" | custom-call | tf_op jit(solution)/shard_map/pallas_call | solution.py:322
  27.4 1.3 %shard_map.87 = (f32[1,256]{1,0:T(1,128)}, f32[8,64]{1,0:T(8,128)}) custom-call(f32[1,256]{1,0:T(1,128)} %get-tuple-element.6.tail_in, f32[8,64]{1,0:T(8,128)} %get-tuple-element.7.cand_in), custom_call_target="tpu_custom_call" | custom-call | tf_op jit(solution)/shard_map/pallas_call | solution.py:362
